TPU v7x, 32 devices: a 4x4x1 block of a 4x4x8 slice. The times are simulated.
32 devices in a mesh: rep: 2 (over z, core), dp: 16 (over x, y).
Axes of the slice: x: 4, y: 4, z: 1, core: 2. Of those that a mesh axis runs over, the one named last changes fastest.
The devices are a block of a 4x4x8 slice.
Arguments:
- g_w_gate: bfloat16 [32, 2, 896, 2560], P(('rep', 'dp')), parts along dimension 0
- g_w_up: bfloat16 [32, 2, 896, 2560], P(('rep', 'dp')), parts along dimension 0
- g_w_down: bfloat16 [32, 2, 2560, 896], P(('rep', 'dp')), parts along dimension 0
- w_gate: bfloat16 [2, 896, 2560], replicated
- w_up: bfloat16 [2, 896, 2560], replicated
- w_down: bfloat16 [2, 2560, 896], replicated
- m_w_gate: float32 [2, 896, 2560], P(None, 'dp')
- m_w_up: float32 [2, 896, 2560], P(None, 'dp')
- m_w_down: float32 [2, 2560, 896], P(None, 'dp')
- v_w_gate: float32 [2, 896, 2560], P(None, 'dp')
- v_w_up: float32 [2, 896, 2560], P(None, 'dp')
- v_w_down: float32 [2, 2560, 896], P(None, 'dp')
Outputs:
- output 1: bfloat16 [4, 896, 2560], P('rep'), parts along dimension 0
- output 2: bfloat16 [4, 896, 2560], P('rep'), parts along dimension 0
- output 3: bfloat16 [4, 2560, 896], P('rep'), parts along dimension 0
- output 4: float32 [4, 896, 2560], P('rep', 'dp'), parts along dimension 0
- output 5: float32 [4, 896, 2560], P('rep', 'dp'), parts along dimension 0
- output 6: float32 [4, 2560, 896], P('rep', 'dp'), parts along dimension 0
- output 7: float32 [4, 896, 2560], P('rep', 'dp'), parts along dimension 0
- output 8: float32 [4, 896, 2560], P('rep', 'dp'), parts along dimension 0
- output 9: float32 [4, 2560, 896], P('rep', 'dp'), parts along dimension 0
There are 2 independent parts. A program takes and returns all parts, laid end to end along the dimension named above; an argument that names none is the same for every part.
All inputs are finite; a program needn't handle non-finite values.
Results may differ from a plain program's by a relative error of at most 0.022.
Values are sent between devices in bfloat16 or wider.
A program may use at most 768 MiB of HBM per device.

v0:
```python
import jax
import jax.numpy as jnp
from jax import lax
from jax.sharding import PartitionSpec as P


def adamw(w, m, v, g):
    m = 0.9 * m + 0.1 * g
    v = 0.95 * v + 0.05 * g * g
    step = m * lax.rsqrt(v + 1e-8) + 0.1 * w
    return (w - 0.02 * step).astype(jnp.bfloat16), m, v


def clipped(gradients, sum_of_squares, count):
    factor = jnp.minimum(1.0, 0.5 * lax.rsqrt(sum_of_squares / count + 1e-30))
    return [g * factor for g in gradients]


def solution(mesh):
    def step(*arrays):
        terms, weights, m, v = (arrays[i : i + 3] for i in (0, 3, 6, 9))
        gradients = [lax.psum_scatter(t[0], "dp", scatter_dimension=1, tiled=True).astype(jnp.float32) for t in terms]
        squares = lax.psum(sum(jnp.sum(g * g) for g in gradients), "dp")
        gradients = clipped(gradients, squares, lax.psum(1, "dp") * sum(g.size for g in gradients))
        me = lax.axis_index("dp")
        own = [lax.dynamic_slice_in_dim(w, me * one.shape[1], one.shape[1], 1).astype(jnp.float32) for w, one in zip(weights, m, strict=True)]
        new = [adamw(w, m, v, g) for w, m, v, g in zip(own, m, v, gradients, strict=True)]
        whole = [lax.all_gather(one[0], "dp", axis=1, tiled=True) for one in new]
        return (*whole, *(one[1] for one in new), *(one[2] for one in new))

    all_of, cut = P(None, None, None), P(None, "dp", None)
    return jax.shard_map(
        step,
        mesh=mesh,
        in_specs=(P(("rep", "dp"), None, None, None),) * 3 + (all_of,) * 3 + (cut,) * 6,
        out_specs=(P("rep", None, None),) * 3 + (P("rep", "dp", None),) * 6,
        check_vma=False,
    )
```

profile of v0, /device:TPU:96, one launch (start us, length us, event | category | flops | bytes accessed | tf_op | source)
XLA Modules:
  0.0 608.7 jit_solution(15461046054424641072)
XLA Ops:
  7.2 0.1 all-reduce.5.cloned.1.call-start
  7.3 0.7 all-reduce.5.cloned.1.call-update
  8.0 0.1 reduce-scatter.4.cloned.1.call-start
  8.1 0.7 reduce-scatter.4.cloned.1.call-update
  8.8 0.1 all-gather.4.cloned.1.call-start
  8.9 0.6 dynamic-slice
  10.1 230.4 %all-reduce.5.cloned.1.call-done = (bf16[2,896,2560]{2,1,0:T(8,128)(2,1)}, bf16[2,896,2560]{2,1,0:T(8,128)(2,1)}) async-done(((bf16[2,896,2560]{2,1,0:T(8,128)(2,1)}, bf16[2,896,2560]{2,1,0:T(8,128)(2,1)}), (bf16[2,896,2560]{2,1,0:T(8,128)(2,1)}, bf16[2,896,2560]{2,1,0:T(8,128)(2,1)})) %all-reduce.5.cloned.1.call-update) | async-done | bytes 18350096
  240.5 2.1 fusion.9
  244.0 81.8 %reduce-scatter.4.cloned.1.call-done = bf16[2,160,896]{2,1,0:T(8,128)(2,1)} async-done(((bf16[2,2560,896]{2,1,0:T(8,128)(2,1)}), bf16[2,160,896]{2,1,0:T(8,128)(2,1)}) %reduce-scatter.4.cloned.1.call-update) | async-done | bytes 573456 | tf_op jit(solution)/shard_map/reduce_scatter | solution.py:22
  325.8 2.0 fusion.11
  328.4 38.7 %psum.7 = f32[]{:T(128)} all-reduce(f32[]{:T(128)S(6)} %add.65), channel_id=1, replica_groups=mesh['rep'=2,'dp'=16] {'dp'}, use_global_device_ids=true, to_apply=%region_6.0 | all-reduce | flops 1 | bytes 8 | tf_op jit(solution)/shard_map/psum | solution.py:23
  367.8 3.2 fusion.8
  371.0 0.1 all-gather.4.cloned.1.call-update
  371.1 0.1 all-gather.6.cloned.1.call-start
  371.2 3.6 fusion.14
  374.8 0.1 all-gather.6.cloned.1.call-update
  374.8 0.1 all-gather.8.cloned.1.call-start
  374.9 3.3 fusion.17
  378.3 57.9 %all-gather.4.cloned.1.call-done = bf16[2,896,2560]{2,1,0:T(8,128)(2,1)} async-done(((bf16[2,56,2560]{2,1,0:T(8,128)(2,1)}), bf16[2,896,2560]{2,1,0:T(8,128)(2,1)}) %all-gather.4.cloned.1.call-update) | async-done | bytes 9175056 | tf_op jit(solution)/shard_map/all_gather | solution.py:28
  436.2 71.2 %all-gather.6.cloned.1.call-done = bf16[2,896,2560]{2,1,0:T(8,128)(2,1)} async-done(((bf16[2,56,2560]{2,1,0:T(8,128)(2,1)}), bf16[2,896,2560]{2,1,0:T(8,128)(2,1)}) %all-gather.6.cloned.1.call-update) | async-done | bytes 9175056 | tf_op jit(solution)/shard_map/all_gather | solution.py:28
  507.3 71.2 %all-gather.8.cloned.1.call-done = bf16[2,2560,896]{2,1,0:T(8,128)(2,1)} async-done(((bf16[2,160,896]{2,1,0:T(8,128)(2,1)}), bf16[2,2560,896]{2,1,0:T(8,128)(2,1)}) %all-gather.8.cloned.1.call-update) | async-done | bytes 9175056 | tf_op jit(solution)/shard_map/all_gather | solution.py:28
  578.5 7.8 %copy.32 = bf16[2,896,2560]{2,1,0:T(8,128)(2,1)} copy(bf16[2,896,2560]{2,1,0:T(8,128)(2,1)} %all-gather.4.cloned.1.call-done) | data formatting | bytes 18350080
  586.4 7.8 %copy.33 = bf16[2,896,2560]{2,1,0:T(8,128)(2,1)} copy(bf16[2,896,2560]{2,1,0:T(8,128)(2,1)} %all-gather.6.cloned.1.call-done) | data formatting | bytes 18350080
  594.2 8.0 %copy.34 = bf16[2,2560,896]{2,1,0:T(8,128)(2,1)} copy(bf16[2,2560,896]{2,1,0:T(8,128)(2,1)} %all-gather.8.cloned.1.call-done) | data formatting | bytes 18350080
  (13 shorter events, 0.1 us)
Async XLA Ops:
  7.2 233.3 %all-reduce.5.cloned.1.call-start = ((), (), s32[]{:S(2)}) async-start(), calls=%async_computation.5 | async-start | bytes 36700160
  8.0 317.8 %reduce-scatter.4.cloned.1.call-start = ((), (), s32[]{:S(2)}) async-start(), calls=%async_computation.1 | async-start | bytes 9748480 | tf_op jit(solution)/shard_map/reduce_scatter | solution.py:22
  8.1 0.8 copy-start.5
  8.1 359.7 %copy-start.2 = (f32[2,56,2560]{2,1,0:T(8,128)S(1)}, f32[2,56,2560]{2,1,0:T(8,128)}, u32[]{:S(2)}) copy-start(f32[2,56,2560]{2,1,0:T(8,128)} %param.18) | copy-start | bytes 3440644
  8.8 359.0 %copy-start.1 = (f32[2,56,2560]{2,1,0:T(8,128)S(1)}, f32[2,56,2560]{2,1,0:T(8,128)}, u32[]{:S(2)}) copy-start(f32[2,56,2560]{2,1,0:T(8,128)} %param.21) | copy-start | bytes 3440644
  8.8 427.4 %all-gather.4.cloned.1.call-start = ((), (), s32[]{:S(2)}) async-start(), calls=%async_computation.2 | async-start | bytes 9748480 | tf_op jit(solution)/shard_map/all_gather | solution.py:28
  367.8 3.4 copy-start.3
  371.1 3.8 copy-start
  371.1 136.3 %all-gather.6.cloned.1.call-start = ((), (), s32[]{:S(2)}) async-start(), calls=%async_computation.3 | async-start | bytes 9748480 | tf_op jit(solution)/shard_map/all_gather | solution.py:28
  371.2 3.8 copy-start.4
  374.8 203.7 %all-gather.8.cloned.1.call-start = ((), (), s32[]{:S(2)}) async-start(), calls=%async_computation.4 | async-start | bytes 9748480 | tf_op jit(solution)/shard_map/all_gather | solution.py:28
Sparse Core Ops, SparseCore 0:
  12.1 228.3 all-reduce.4
  243.8 81.9 reduce-scatter.3
  371.2 64.9 all-gather.3
  438.6 68.7 all-gather.5
  509.7 68.7 all-gather.7
where the time goes:
time: 610 us; the launch traced here: 609 us
  waiting for transfers between devices  514 us (84%)
  blocking collectives  38.7 us (6%)
  local copies, waits for them, and re-layouts  24.3 us (4%)
  between operations  17.2 us (3%)
  other arithmetic  14.2 us (2%)
    unnamed x6, waiting for transfers between devices  232 us
    all_gather x3, waiting for transfers between devices, step(): whole = [lax.all_gather(one[0], 'dp', axis=1, tiled=True) for one in new]  200 us
    reduce_scatter x1, waiting for transfers between devices, step(): lax.psum_scatter(t[0], 'dp', scatter_dimension=1, tiled=True)  81.8 us
    psum x1, blocking collectives, step(): squares = lax.psum(sum((jnp.sum(g * g) for g in gradients)), 'dp')  38.7 us
    unnamed x16, local copies, waits for them, and re-layouts  24.3 us
  transfers between devices with their start and end apart: 5, of which 5 were waited for; matrix products, arithmetic and copies ran while one was open for 2% of the time, Pallas kernels for 0%

commit v1 on v0

v1 whole, which is shorter than its diff:
```python
import functools
import math

import jax
import jax.numpy as jnp
from jax import lax
from jax.experimental import pallas as pl
from jax.experimental.pallas import tpu as pltpu
from jax.sharding import PartitionSpec as P

MESH = pl.DeviceIdType.MESH
COLOURS = 4


def tiled(a, lead):
    rows, columns = a.shape[-2:]
    t = a.reshape(*a.shape[:-2], rows // 8, 8, columns // 128, 128)
    return jnp.swapaxes(t, -3, -2).reshape(*lead, -1, 8, 128)


def untiled(t, shape):
    rows, columns = shape[-2:]
    t = t.reshape(*shape[:-2], rows // 8, columns // 128, 8, 128)
    return jnp.swapaxes(t, -3, -2).reshape(shape)


def step_kernel(side, layers, count, *refs):
    n = side * side
    terms, weights, m_in, v_in = (refs[i : i + 3] for i in (0, 3, 6, 9))
    whole, m_ref, v_ref, first, second, own_w, squares, total, load, load3, send, recv, sq_send, sq_recv = refs[12:]
    pieces = whole.shape[0]
    tiles = whole.shape[3]
    part = tiles // COLOURS
    hops = side - 1
    me = lax.axis_index("dp")
    x, y = me // side, me % side

    def load_terms(piece):
        return pltpu.make_async_copy(terms[piece // layers].at[piece % layers], whole.at[piece], load.at[piece])

    def load_state(piece):
        a, l = piece // layers, piece % layers
        return (
            pltpu.make_async_copy(weights[a].at[l, x, y], own_w.at[piece], load3.at[0, piece]),
            pltpu.make_async_copy(m_in[a].at[l], m_ref.at[piece], load3.at[1, piece]),
            pltpu.make_async_copy(v_in[a].at[l], v_ref.at[piece], load3.at[2, piece]),
        )

    for piece in range(pieces):
        load_terms(piece).start()

    barrier = pltpu.get_barrier_semaphore()

    @pl.loop(1, n)
    def _(i):
        pl.semaphore_signal(barrier, inc=1, device_id={"dp": (me + i) % n}, device_id_type=MESH)

    pl.semaphore_wait(barrier, n - 1)

    def place(c):
        way = 1 if c % 2 == 0 else -1
        return (x, y, way) if c < 2 else (y, x, way)

    def device(c, p, q):
        return p * side + q if c < 2 else q * side + p

    def row(c, piece, p):
        cut = pl.ds(c * part, part)
        return whole.at[piece, p, :, cut] if c < 2 else whole.at[piece, :, p, cut]

    def block(c, piece, p, q):
        cut = pl.ds(c * part, part)
        return whole.at[piece, p, q, cut] if c < 2 else whole.at[piece, q, p, cut]

    def wrap(i):
        return (i + 2 * side) % side

    def scatter(c, k, piece):
        p, q, way = place(c)
        if k < hops:
            source, target = row(c, piece, wrap(p - way * (k + 1))), first.at[k, c, piece]
            to = device(c, wrap(p + way), q)
        else:
            source, target = block(c, piece, p, wrap(q - way * (k - hops + 1))), second.at[k - hops, c, piece]
            to = device(c, p, wrap(q + way))
        return pltpu.make_async_remote_copy(
            src_ref=source, dst_ref=target, send_sem=send.at[k, c, piece], recv_sem=recv.at[k, c, piece], device_id={"dp": to}, device_id_type=MESH
        )

    def add(c, k, piece):
        p, q, way = place(c)
        if k < hops:
            mine, came = row(c, piece, wrap(p - way * (k + 2))), first.at[k, c, piece]

            @pl.loop(0, side)
            def _(i):
                mine[i] = (mine[i].astype(jnp.float32) + came[i].astype(jnp.float32)).astype(jnp.bfloat16)

        else:
            mine, came = block(c, piece, p, wrap(q - way * (k - hops + 2))), second.at[k - hops, c, piece]
            new = (mine[...].astype(jnp.float32) + came[...].astype(jnp.float32)).astype(jnp.bfloat16)
            mine[...] = new
            if k == 2 * hops - 1:
                g = new.astype(jnp.float32)
                total[...] += jnp.sum(g * g, axis=0)

    total[...] = jnp.zeros_like(total)

    for piece in range(pieces):
        load_terms(piece).wait()
        for c in range(COLOURS):
            scatter(c, 0, piece).start()
    for piece in range(pieces):
        for copy in load_state(piece):
            copy.start()

    last = COLOURS - 1
    for k in range(2 * hops):

        @pl.loop(0, pieces)
        def _(piece, k=k):
            for c in range(COLOURS):
                scatter(c, k, piece).wait_recv()
                add(c, k, piece)
                if c:
                    if k + 1 < 2 * hops:
                        scatter(c - 1, k + 1, piece).start()
                    continue

                if k + 1 < 2 * hops:

                    @pl.when(piece > 0)
                    def _():
                        scatter(last, k + 1, piece - 1).start()

                if k:

                    @pl.when(piece == 0)
                    def _():
                        scatter(last, k, pieces - 1).start()

    for k in range(2 * hops):

        @pl.loop(0, pieces)
        def _(piece, k=k):
            for c in range(COLOURS):
                scatter(c, k, piece).wait_send()

    def tell(i):
        return pltpu.make_async_remote_copy(
            src_ref=total, dst_ref=squares.at[i], send_sem=sq_send.at[i], recv_sem=sq_recv.at[i], device_id={"dp": (me + i) % n}, device_id_type=MESH
        )

    @pl.loop(1, n)
    def _(i):
        tell(i).start()

    squares[0] = total[...]
    for piece in range(pieces):
        for copy in load_state(piece):
            copy.wait()

    @pl.loop(1, n)
    def _(i):
        tell(i).wait_recv()

    of_all = jnp.sum(jnp.sum(squares[...], axis=0), keepdims=True)
    factor = jnp.minimum(1.0, 0.5 * lax.rsqrt(of_all / count + 1e-30))[None]

    def gather(c, k, piece):
        p, q, way = place(c)
        if k < hops:
            moved, to = block(c, piece, p, wrap(q - way * k)), device(c, p, wrap(q + way))
        else:
            moved, to = row(c, piece, wrap(p - way * (k - hops))), device(c, wrap(p + way), q)
        return pltpu.make_async_remote_copy(
            src_ref=moved, dst_ref=moved, send_sem=send.at[k, c, piece], recv_sem=recv.at[k, c, piece], device_id={"dp": to}, device_id_type=MESH
        )

    @pl.loop(0, pieces)
    def _(piece):
        mine = whole.at[piece, x, y]

        @pl.loop(0, COLOURS)
        def _(c):
            cut = pl.ds(c * part, part)
            g = mine[cut].astype(jnp.float32) * factor
            w = own_w[piece, cut].astype(jnp.float32)
            m = 0.9 * m_ref[piece, cut] + 0.1 * g
            v = 0.95 * v_ref[piece, cut] + 0.05 * g * g
            m_ref[piece, cut] = m
            v_ref[piece, cut] = v
            mine[cut] = (w - 0.02 * (m * lax.rsqrt(v + 1e-8) + 0.1 * w)).astype(jnp.bfloat16)

        @pl.when(piece > 0)
        def _():
            for c in range(COLOURS):
                gather(c, 0, piece - 1).start()

    for k in range(2 * hops):

        @pl.loop(0, pieces)
        def _(piece, k=k):
            for c in range(COLOURS):
                gather(c, k, piece).wait_recv()
                if k + 1 < 2 * hops:
                    gather(c, k + 1, piece).start()
            if k == 0:

                @pl.when(piece == 0)
                def _():
                    for c in range(COLOURS):
                        gather(c, 0, pieces - 1).start()

    for k in range(2 * hops):

        @pl.loop(0, pieces)
        def _(piece, k=k):
            for c in range(COLOURS):
                gather(c, k, piece).wait_send()

    @pl.loop(1, n)
    def _(i):
        tell(i).wait_send()


def out_kernel(layers, whole, m_ref, v_ref, *refs):
    outs, sems = refs[:9], refs[9]
    copies = [
        pltpu.make_async_copy(source.at[3 * 0 + piece], outs[3 * i + piece // layers].at[piece % layers], sems.at[i, piece])
        for i, source in enumerate((whole, m_ref, v_ref))
        for piece in range(3 * layers)
    ]
    for copy in copies:
        copy.start()
    for copy in copies:
        copy.wait()


def solution(mesh):
    n = mesh.shape["dp"]
    side = math.isqrt(n)

    def step(*arrays):
        terms, weights, m, v = (arrays[i : i + 3] for i in (0, 3, 6, 9))
        layers = weights[0].shape[0]
        pieces = 3 * layers
        terms = [tiled(t[0], (layers, side, side)) for t in terms]
        whole = [tiled(w, (layers, side, side)) for w in weights]
        ms = [tiled(one, (layers,)) for one in m]
        vs = [tiled(one, (layers,)) for one in v]
        tiles = ms[0].shape[1]
        part = tiles // COLOURS
        assert side * side == n and tiles % COLOURS == 0 and all(one.shape[1] == tiles for one in ms)
        hops = side - 1
        any_space = pl.BlockSpec(memory_space=pl.ANY)
        vmem = pl.BlockSpec(memory_space=pltpu.VMEM)
        bf16, f32, dma = jnp.bfloat16, jnp.float32, pltpu.SemaphoreType.DMA
        count = float(sum(w.size for w in weights))
        new = pl.pallas_call(
            functools.partial(step_kernel, side, layers, count),
            out_shape=(
                pltpu.VMEM((pieces, side, side, tiles, 8, 128), bf16),
                pltpu.VMEM((pieces, tiles, 8, 128), f32),
                pltpu.VMEM((pieces, tiles, 8, 128), f32),
            ),
            in_specs=[any_space] * 12,
            out_specs=(vmem,) * 3,
            scratch_shapes=[
                pltpu.VMEM((hops, COLOURS, pieces, side, part, 8, 128), bf16),
                pltpu.VMEM((hops, COLOURS, pieces, part, 8, 128), bf16),
                pltpu.VMEM((pieces, tiles, 8, 128), bf16),
                pltpu.VMEM((n, 8, 128), f32),
                pltpu.VMEM((8, 128), f32),
                dma((pieces,)),
                dma((3, pieces)),
                dma((2 * hops, COLOURS, pieces)),
                dma((2 * hops, COLOURS, pieces)),
                dma((n,)),
                dma((n,)),
            ],
            compiler_params=pltpu.CompilerParams(collective_id=0, has_side_effects=True, vmem_limit_bytes=27 * 2**20),
            name="step",
        )(*terms, *whole, *ms, *vs)
        return finish(new, layers, weights, m, v)
        shapes = [(layers, side, side, tiles, 8, 128)] * 3 + [(layers, tiles, 8, 128)] * 6
        outs = pl.pallas_call(
            functools.partial(out_kernel, layers),
            out_shape=[jax.ShapeDtypeStruct(s, bf16 if i < 3 else f32) for i, s in enumerate(shapes)],
            in_specs=[vmem] * 3,
            out_specs=[any_space] * 9,
            scratch_shapes=[dma((3, pieces))],
            compiler_params=pltpu.CompilerParams(vmem_limit_bytes=2**20),
            name="out",
        )(*new)
        return tuple(untiled(one, like.shape) for one, like in zip(outs, (*weights, *m, *v), strict=True))

    all_of, cut = P(None, None, None), P(None, "dp", None)
    return jax.shard_map(
        step,
        mesh=mesh,
        in_specs=(P(("rep", "dp"), None, None, None),) * 3 + (all_of,) * 3 + (cut,) * 6,
        out_specs=(P("rep", None, None),) * 3 + (P("rep", "dp", None),) * 6,
        check_vma=False,
    )

def finish(new, layers, weights, m, v):
    outs = [one[layers * a : layers * (a + 1)] for one in new for a in range(3)]
    return tuple(untiled(one, like.shape) for one, like in zip(outs, (*weights, *m, *v), strict=True))
```

time: 610 us -> 331 us (0.54)
  waiting for transfers between devices: 514 us -> 0 us
  Pallas kernels: 0 us -> 296 us
  blocking collectives: 38.7 us -> 0 us
  between operations: 17.2 us -> 0.66 us
  other arithmetic: 14.2 us -> 0 us
  local copies, waits for them, and re-layouts: 24.3 us -> 34.4 us
    pallas_call x0 -> x1, Pallas kernels: none -> 296 us  [step(): pl.pallas_call(functools.partial(step_kernel, side, layers, count), out_s...]
    unnamed x6 -> x0, waiting for transfers between devices: 232 us -> none
    all_gather x3 -> x0, waiting for transfers between devices: 200 us -> none  [step(): whole = [lax.all_gather(one[0], 'dp', axis=1, tiled=True) for one in new]]
    reduce_scatter x1 -> x0, waiting for transfers between devices: 81.8 us -> none  [step(): lax.psum_scatter(t[0], 'dp', scatter_dimension=1, tiled=True)]
    psum x1 -> x0, blocking collectives: 38.7 us -> none  [step(): squares = lax.psum(sum((jnp.sum(g * g) for g in gradients)), 'dp')]
    slice x0 -> x2, local copies, waits for them, and re-layouts: none -> 25.3 us  [finish(): outs = [one[layers * a:layers * (a + 1)] for one in new for a in range(3)]]
    unnamed x16 -> x2, local copies, waits for them, and re-layouts: 24.3 us -> 9.07 us
    convert_element_type x3 -> x0, other arithmetic: 10.1 us -> none  [adamw(): return ((w - 0.02 * step).astype(jnp.bfloat16), m, v)]
  transfers between devices with their start and end apart: 5 -> 0, of which waited for: 5 -> 0; matrix products, arithmetic and copies ran while one was open for 2% -> 0% of each run, Pallas kernels for 0% -> 0%
where the time goes in v1:
time: 331 us
  Pallas kernels  296 us (89%)
  local copies, waits for them, and re-layouts  34.4 us (10%)
    pallas_call x1, Pallas kernels, step(): pl.pallas_call(functools.partial(step_kernel, side, layers, count), out_s...  296 us
    slice x2, local copies, waits for them, and re-layouts, finish(): outs = [one[layers * a:layers * (a + 1)] for one in new for a in range(3)]  25.3 us
    unnamed x2, local copies, waits for them, and re-layouts  9.07 us

profile of v1, /device:TPU:96, one launch (start us, length us, event | category | flops | bytes accessed | tf_op | source)
XLA Modules:
  0.0 330.9 jit_solution(2313255686642771354)
XLA Ops:
  0.6 295.9 %step.1 = (bf16[6,4,4,140,8,128]{5,4,3,2,1,0:T(8,128)(2,1)S(1)}, f32[6,140,8,128]{3,2,1,0:T(8,128)S(1)}, f32[6,140,8,128]{3,2,1,0:T(8,128)S(1)}) custom-call(bf16[2,4,4,140,8,128]{5,4,3,2,1,0:T(8,128)(2,1)} %bitcast.108, bf16[2,4,4,140,8,128]{5,4,3,2,1,0:T(8,128)(2,1)} %bitcast.109, bf16[2,4,4,140,8,128]{5,4,3,2,1,0:T(8,128)(2,1)} %bitcast.110, ...), custom_call_target="tpu_custom_call" | custom-call | tf_op jit(solution)/shard_map/step/pallas_call | solution.py:260
  296.5 0.0 copy-start
  296.5 9.1 %copy-done = bf16[6,4,4,140,8,128]{5,4,3,2,1,0:T(8,128)(2,1)} copy-done((bf16[6,4,4,140,8,128]{5,4,3,2,1,0:T(8,128)(2,1)}, bf16[6,4,4,140,8,128]{5,4,3,2,1,0:T(8,128)(2,1)S(1)}, u32[]{:S(2)}) %copy-start) | copy-done | bytes 27525144
  305.6 22.4 %fusion = (bf16[2,4,4,140,8,128]{5,4,3,2,1,0:T(8,128)(2,1)}, bf16[2,4,4,140,8,128]{5,4,3,2,1,0:T(8,128)(2,1)}, bf16[2,4,4,140,8,128]{5,4,3,2,1,0:T(8,128)(2,1)}) fusion(bf16[6,4,4,140,8,128]{5,4,3,2,1,0:T(8,128)(2,1)} %copy-done), kind=kLoop, calls=%fused_computation | loop fusion | bytes 55050240 | tf_op jit(solution)/shard_map/slice | solution.py:308
  328.0 2.9 fusion.1
Async XLA Ops:
  296.5 9.1 %copy-start = (bf16[6,4,4,140,8,128]{5,4,3,2,1,0:T(8,128)(2,1)}, bf16[6,4,4,140,8,128]{5,4,3,2,1,0:T(8,128)(2,1)S(1)}, u32[]{:S(2)}) copy-start(bf16[6,4,4,140,8,128]{5,4,3,2,1,0:T(8,128)(2,1)S(1)} %get-tuple-element.12) | copy-start | bytes 82575360

commit v2 on v1

--- a/solution.py
+++ b/solution.py
@@ -27,7 +27,8 @@
 def step_kernel(side, layers, count, *refs):
     n = side * side
     terms, weights, m_in, v_in = (refs[i : i + 3] for i in (0, 3, 6, 9))
-    whole, m_ref, v_ref, first, second, own_w, squares, total, load, load3, send, recv, sq_send, sq_recv = refs[12:]
+    state, whole, first, second, own_w, squares, total, load, load3, send, recv, sq_send, sq_recv = refs[12:]
+    m_ref, v_ref = state.at[0], state.at[1]
     pieces = whole.shape[0]
     tiles = whole.shape[3]
     part = tiles // COLOURS
@@ -224,11 +225,11 @@
         tell(i).wait_send()
 
 
-def out_kernel(layers, whole, m_ref, v_ref, *refs):
+def out_kernel(layers, state, whole, *refs):
     outs, sems = refs[:9], refs[9]
     copies = [
-        pltpu.make_async_copy(source.at[3 * 0 + piece], outs[3 * i + piece // layers].at[piece % layers], sems.at[i, piece])
-        for i, source in enumerate((whole, m_ref, v_ref))
+        pltpu.make_async_copy(source.at[piece], outs[3 * i + piece // layers].at[piece % layers], sems.at[i, piece])
+        for i, source in enumerate((whole, state.at[0], state.at[1]))
         for piece in range(3 * layers)
     ]
     for copy in copies:
@@ -260,12 +261,11 @@
         new = pl.pallas_call(
             functools.partial(step_kernel, side, layers, count),
             out_shape=(
+                pltpu.VMEM((2, pieces, tiles, 8, 128), f32),
                 pltpu.VMEM((pieces, side, side, tiles, 8, 128), bf16),
-                pltpu.VMEM((pieces, tiles, 8, 128), f32),
-                pltpu.VMEM((pieces, tiles, 8, 128), f32),
             ),
             in_specs=[any_space] * 12,
-            out_specs=(vmem,) * 3,
+            out_specs=(vmem,) * 2,
             scratch_shapes=[
                 pltpu.VMEM((hops, COLOURS, pieces, side, part, 8, 128), bf16),
                 pltpu.VMEM((hops, COLOURS, pieces, part, 8, 128), bf16),
@@ -282,12 +282,12 @@
             compiler_params=pltpu.CompilerParams(collective_id=0, has_side_effects=True, vmem_limit_bytes=27 * 2**20),
             name="step",
         )(*terms, *whole, *ms, *vs)
-        return finish(new, layers, weights, m, v)
+        new = [pltpu.with_memory_space_constraint(one, pltpu.VMEM) for one in new]
         shapes = [(layers, side, side, tiles, 8, 128)] * 3 + [(layers, tiles, 8, 128)] * 6
         outs = pl.pallas_call(
             functools.partial(out_kernel, layers),
             out_shape=[jax.ShapeDtypeStruct(s, bf16 if i < 3 else f32) for i, s in enumerate(shapes)],
-            in_specs=[vmem] * 3,
+            in_specs=[vmem] * 2,
             out_specs=[any_space] * 9,
             scratch_shapes=[dma((3, pieces))],
             compiler_params=pltpu.CompilerParams(vmem_limit_bytes=2**20),
@@ -303,7 +303,3 @@
         out_specs=(P("rep", None, None),) * 3 + (P("rep", "dp", None),) * 6,
         check_vma=False,
     )
-
-def finish(new, layers, weights, m, v):
-    outs = [one[layers * a : layers * (a + 1)] for one in new for a in range(3)]
-    return tuple(untiled(one, like.shape) for one, like in zip(outs, (*weights, *m, *v), strict=True))

time: 331 us -> 308 us (0.931)
  local copies, waits for them, and re-layouts: 34.4 us -> 0 us
  Pallas kernels: 296 us -> 307 us
    slice x2 -> x0, local copies, waits for them, and re-layouts: 25.3 us -> none  [finish(): outs = [one[layers * a:layers * (a + 1)] for one in new for a in range(3)]]
    pallas_call x0 -> x1, Pallas kernels: none -> 11.3 us  [step(): pl.pallas_call(functools.partial(out_kernel, layers), out_shape=[jax.Shap...]
    unnamed x2 -> x0, local copies, waits for them, and re-layouts: 9.07 us -> none
where the time goes in v2:
time: 308 us
  Pallas kernels  307 us (100%)
    pallas_call x1, Pallas kernels, step(): pl.pallas_call(functools.partial(step_kernel, side, layers, count), out_s...  296 us
    pallas_call x1, Pallas kernels, step(): pl.pallas_call(functools.partial(out_kernel, layers), out_shape=[jax.Shap...  11.3 us

profile of v2, /device:TPU:96, one launch (start us, length us, event | category | flops | bytes accessed | tf_op | source)
XLA Modules:
  0.0 307.8 jit_solution(8064144964353893193)
XLA Ops:
  0.6 295.9 %step.1 = (f32[2,6,140,8,128]{4,3,2,1,0:T(8,128)S(1)}, bf16[6,4,4,140,8,128]{5,4,3,2,1,0:T(8,128)(2,1)S(1)}) custom-call(bf16[2,4,4,140,8,128]{5,4,3,2,1,0:T(8,128)(2,1)} %bitcast.105, bf16[2,4,4,140,8,128]{5,4,3,2,1,0:T(8,128)(2,1)} %bitcast.106, bf16[2,4,4,140,8,128]{5,4,3,2,1,0:T(8,128)(2,1)} %bitcast.107, bf16[2,4,4,140,8,128]{5,4,3,2,1,0:T(8,128)(2,1)} %bitcast.108, ...), custom_call_target="tpu_custom_call" | custom-call | tf_op jit(solution)/shard_map/step/pallas_call | solution.py:261
  296.5 11.3 %out.1 = (bf16[2,4,4,140,8,128]{5,4,3,2,1,0:T(8,128)(2,1)}, bf16[2,4,4,140,8,128]{5,4,3,2,1,0:T(8,128)(2,1)}, bf16[2,4,4,140,8,128]{5,4,3,2,1,0:T(8,128)(2,1)}, ...) custom-call(f32[2,6,140,8,128]{4,3,2,1,0:T(8,128)S(1)} %get-tuple-el, ...), custom_call_target="tpu_custom_call" | custom-call | tf_op jit(solution)/shard_map/out/pallas_call | solution.py:287

commit v3 on v2

--- a/solution.py
+++ b/solution.py
@@ -52,12 +52,6 @@
 
     barrier = pltpu.get_barrier_semaphore()
 
-    @pl.loop(1, n)
-    def _(i):
-        pl.semaphore_signal(barrier, inc=1, device_id={"dp": (me + i) % n}, device_id_type=MESH)
-
-    pl.semaphore_wait(barrier, n - 1)
-
     def place(c):
         way = 1 if c % 2 == 0 else -1
         return (x, y, way) if c < 2 else (y, x, way)
@@ -65,6 +59,11 @@
     def device(c, p, q):
         return p * side + q if c < 2 else q * side + p
 
+    for c in range(COLOURS):
+        p, q, way = place(c)
+        pl.semaphore_signal(barrier, inc=1, device_id={"dp": device(c, (p + way + side) % side, q)}, device_id_type=MESH)
+    pl.semaphore_wait(barrier, COLOURS)
+
     def row(c, piece, p):
         cut = pl.ds(c * part, part)
         return whole.at[piece, p, :, cut] if c < 2 else whole.at[piece, :, p, cut]
@@ -76,11 +75,15 @@
     def wrap(i):
         return (i + 2 * side) % side
 
-    def scatter(c, k, piece):
+    def scatter(c, k, piece, own=None):
         p, q, way = place(c)
         if k < hops:
             source, target = row(c, piece, wrap(p - way * (k + 1))), first.at[k, c, piece]
             to = device(c, wrap(p + way), q)
+            if own is not None:
+                cut = pl.ds(c * part, part)
+                own, i = own.at[piece % layers], wrap(p - way)
+                source = own.at[i, :, cut] if c < 2 else own.at[:, i, cut]
         else:
             source, target = block(c, piece, p, wrap(q - way * (k - hops + 1))), second.at[k - hops, c, piece]
             to = device(c, p, wrap(q + way))
@@ -108,9 +111,8 @@
     total[...] = jnp.zeros_like(total)
 
     for piece in range(pieces):
-        load_terms(piece).wait()
         for c in range(COLOURS):
-            scatter(c, 0, piece).start()
+            scatter(c, 0, piece, terms[piece // layers]).start()
     for piece in range(pieces):
         for copy in load_state(piece):
             copy.start()
@@ -120,9 +122,13 @@
 
         @pl.loop(0, pieces)
         def _(piece, k=k):
+            if k == 0:
+                pltpu.make_async_copy(whole.at[piece], whole.at[piece], load.at[piece]).wait()
             for c in range(COLOURS):
                 scatter(c, k, piece).wait_recv()
                 add(c, k, piece)
+                if k:
+                    scatter(c, k - 1, piece).wait_send()
                 if c:
                     if k + 1 < 2 * hops:
                         scatter(c - 1, k + 1, piece).start()
@@ -140,13 +146,6 @@
                     def _():
                         scatter(last, k, pieces - 1).start()
 
-    for k in range(2 * hops):
-
-        @pl.loop(0, pieces)
-        def _(piece, k=k):
-            for c in range(COLOURS):
-                scatter(c, k, piece).wait_send()
-
     def tell(i):
         return pltpu.make_async_remote_copy(
             src_ref=total, dst_ref=squares.at[i], send_sem=sq_send.at[i], recv_sem=sq_recv.at[i], device_id={"dp": (me + i) % n}, device_id_type=MESH
@@ -157,6 +156,12 @@
         tell(i).start()
 
     squares[0] = total[...]
+
+    @pl.loop(0, pieces)
+    def _(piece):
+        for c in range(COLOURS):
+            scatter(c, 2 * hops - 1, piece).wait_send()
+
     for piece in range(pieces):
         for copy in load_state(piece):
             copy.wait()
@@ -181,9 +186,7 @@
     @pl.loop(0, pieces)
     def _(piece):
         mine = whole.at[piece, x, y]
-
-        @pl.loop(0, COLOURS)
-        def _(c):
+        for c in range(COLOURS):
             cut = pl.ds(c * part, part)
             g = mine[cut].astype(jnp.float32) * factor
             w = own_w[piece, cut].astype(jnp.float32)
@@ -192,11 +195,13 @@
             m_ref[piece, cut] = m
             v_ref[piece, cut] = v
             mine[cut] = (w - 0.02 * (m * lax.rsqrt(v + 1e-8) + 0.1 * w)).astype(jnp.bfloat16)
-
-        @pl.when(piece > 0)
-        def _():
-            for c in range(COLOURS):
-                gather(c, 0, piece - 1).start()
+            if c:
+                gather(c - 1, 0, piece).start()
+            else:
+
+                @pl.when(piece > 0)
+                def _():
+                    gather(last, 0, piece - 1).start()
 
     for k in range(2 * hops):
 
@@ -206,19 +211,18 @@
                 gather(c, k, piece).wait_recv()
                 if k + 1 < 2 * hops:
                     gather(c, k + 1, piece).start()
+                if k:
+                    gather(c, k - 1, piece).wait_send()
             if k == 0:
 
                 @pl.when(piece == 0)
                 def _():
-                    for c in range(COLOURS):
-                        gather(c, 0, pieces - 1).start()
-
-    for k in range(2 * hops):
-
-        @pl.loop(0, pieces)
-        def _(piece, k=k):
-            for c in range(COLOURS):
-                gather(c, k, piece).wait_send()
+                    gather(last, 0, pieces - 1).start()
+
+    @pl.loop(0, pieces)
+    def _(piece):
+        for c in range(COLOURS):
+            gather(c, 2 * hops - 1, piece).wait_send()
 
     @pl.loop(1, n)
     def _(i):

time: 308 us -> 305 us (level)
  no operation moved by 1% of the time
where the time goes in v3:
time: 305 us
  Pallas kernels  305 us (100%)
    pallas_call x1, Pallas kernels, step(): pl.pallas_call(functools.partial(step_kernel, side, layers, count), out_s...  293 us
    pallas_call x1, Pallas kernels, step(): pl.pallas_call(functools.partial(out_kernel, layers), out_shape=[jax.Shap...  11.3 us

profile of v3, /device:TPU:96, one launch (start us, length us, event | category | flops | bytes accessed | tf_op | source)
XLA Modules:
  0.0 305.2 jit_solution(1468330876077960096)
XLA Ops:
  0.6 293.3 %step.1 = (f32[2,6,140,8,128]{4,3,2,1,0:T(8,128)S(1)}, bf16[6,4,4,140,8,128]{5,4,3,2,1,0:T(8,128)(2,1)S(1)}) custom-call(bf16[2,4,4,140,8,128]{5,4,3,2,1,0:T(8,128)(2,1)} %bitcast.105, bf16[2,4,4,140,8,128]{5,4,3,2,1,0:T(8,128)(2,1)} %bitcast.106, bf16[2,4,4,140,8,128]{5,4,3,2,1,0:T(8,128)(2,1)} %bitcast.107, bf16[2,4,4,140,8,128]{5,4,3,2,1,0:T(8,128)(2,1)} %bitcast.108, ...), custom_call_target="tpu_custom_call" | custom-call | tf_op jit(solution)/shard_map/step/pallas_call | solution.py:265
  294.0 11.3 %out.1 = (bf16[2,4,4,140,8,128]{5,4,3,2,1,0:T(8,128)(2,1)}, bf16[2,4,4,140,8,128]{5,4,3,2,1,0:T(8,128)(2,1)}, bf16[2,4,4,140,8,128]{5,4,3,2,1,0:T(8,128)(2,1)}, ...) custom-call(f32[2,6,140,8,128]{4,3,2,1,0:T(8,128)S(1)} %get-tuple-el, ...), custom_call_target="tpu_custom_call" | custom-call | tf_op jit(solution)/shard_map/out/pallas_call | solution.py:291

commit v4 on v3

--- a/solution.py
+++ b/solution.py
@@ -9,6 +9,7 @@
 from jax.sharding import PartitionSpec as P
 
 MESH = pl.DeviceIdType.MESH
+LATE_NS = 13_000
 COLOURS = 4
 
 
@@ -37,14 +38,14 @@
     x, y = me // side, me % side
 
     def load_terms(piece):
-        return pltpu.make_async_copy(terms[piece // layers].at[piece % layers], whole.at[piece], load.at[piece])
+        return pltpu.make_async_copy(terms[piece // layers].at[piece % layers], whole.at[piece], load.at[0])
 
     def load_state(piece):
         a, l = piece // layers, piece % layers
         return (
-            pltpu.make_async_copy(weights[a].at[l, x, y], own_w.at[piece], load3.at[0, piece]),
-            pltpu.make_async_copy(m_in[a].at[l], m_ref.at[piece], load3.at[1, piece]),
-            pltpu.make_async_copy(v_in[a].at[l], v_ref.at[piece], load3.at[2, piece]),
+            pltpu.make_async_copy(weights[a].at[l, x, y], own_w.at[piece], load3.at[0]),
+            pltpu.make_async_copy(m_in[a].at[l], m_ref.at[piece], load3.at[1]),
+            pltpu.make_async_copy(v_in[a].at[l], v_ref.at[piece], load3.at[1]),
         )
 
     for piece in range(pieces):
@@ -88,8 +89,12 @@
             source, target = block(c, piece, p, wrap(q - way * (k - hops + 1))), second.at[k - hops, c, piece]
             to = device(c, p, wrap(q + way))
         return pltpu.make_async_remote_copy(
-            src_ref=source, dst_ref=target, send_sem=send.at[k, c, piece], recv_sem=recv.at[k, c, piece], device_id={"dp": to}, device_id_type=MESH
-        )
+            src_ref=source, dst_ref=target, send_sem=send.at[k], recv_sem=recv.at[k, piece], device_id={"dp": to}, device_id_type=MESH
+        )
+
+    def landed(sem, *those):
+        for one in those:
+            pltpu.make_async_copy(one, one, sem).wait()
 
     def add(c, k, piece):
         p, q, way = place(c)
@@ -110,6 +115,10 @@
 
     total[...] = jnp.zeros_like(total)
 
+    @pl.when(lax.axis_index("rep") % 2 == 0)
+    def _():
+        pl.delay(LATE_NS)
+
     for piece in range(pieces):
         for c in range(COLOURS):
             scatter(c, 0, piece, terms[piece // layers]).start()
@@ -118,17 +127,14 @@
             copy.start()
 
     last = COLOURS - 1
+    landed(load.at[0], whole)
     for k in range(2 * hops):
 
         @pl.loop(0, pieces)
         def _(piece, k=k):
-            if k == 0:
-                pltpu.make_async_copy(whole.at[piece], whole.at[piece], load.at[piece]).wait()
+            landed(recv.at[k, piece], first.at[k, :, piece] if k < hops else second.at[k - hops, :, piece])
             for c in range(COLOURS):
-                scatter(c, k, piece).wait_recv()
                 add(c, k, piece)
-                if k:
-                    scatter(c, k - 1, piece).wait_send()
                 if c:
                     if k + 1 < 2 * hops:
                         scatter(c - 1, k + 1, piece).start()
@@ -146,9 +152,12 @@
                     def _():
                         scatter(last, k, pieces - 1).start()
 
+    for k in range(2 * hops - 1):
+        landed(send.at[k], first.at[k] if k < hops else second.at[k - hops])
+
     def tell(i):
         return pltpu.make_async_remote_copy(
-            src_ref=total, dst_ref=squares.at[i], send_sem=sq_send.at[i], recv_sem=sq_recv.at[i], device_id={"dp": (me + i) % n}, device_id_type=MESH
+            src_ref=total, dst_ref=squares.at[i], send_sem=sq_send.at[0], recv_sem=sq_recv.at[0], device_id={"dp": (me + i) % n}, device_id_type=MESH
         )
 
     @pl.loop(1, n)
@@ -157,18 +166,10 @@
 
     squares[0] = total[...]
 
-    @pl.loop(0, pieces)
-    def _(piece):
-        for c in range(COLOURS):
-            scatter(c, 2 * hops - 1, piece).wait_send()
-
-    for piece in range(pieces):
-        for copy in load_state(piece):
-            copy.wait()
-
-    @pl.loop(1, n)
-    def _(i):
-        tell(i).wait_recv()
+    landed(send.at[2 * hops - 1], second.at[hops - 1])
+    landed(load3.at[0], own_w)
+    landed(load3.at[1], state)
+    landed(sq_recv.at[0], squares.at[pl.ds(1, n - 1)])
 
     of_all = jnp.sum(jnp.sum(squares[...], axis=0), keepdims=True)
     factor = jnp.minimum(1.0, 0.5 * lax.rsqrt(of_all / count + 1e-30))[None]
@@ -180,7 +181,7 @@
         else:
             moved, to = row(c, piece, wrap(p - way * (k - hops))), device(c, wrap(p + way), q)
         return pltpu.make_async_remote_copy(
-            src_ref=moved, dst_ref=moved, send_sem=send.at[k, c, piece], recv_sem=recv.at[k, c, piece], device_id={"dp": to}, device_id_type=MESH
+            src_ref=moved, dst_ref=moved, send_sem=send.at[k], recv_sem=recv.at[k, piece], device_id={"dp": to}, device_id_type=MESH
         )
 
     @pl.loop(0, pieces)
@@ -203,43 +204,97 @@
                 def _():
                     gather(last, 0, piece - 1).start()
 
+    early = pieces - layers
     for k in range(2 * hops):
 
-        @pl.loop(0, pieces)
+        @pl.loop(0, pieces if k < hops else early)
         def _(piece, k=k):
-            for c in range(COLOURS):
-                gather(c, k, piece).wait_recv()
-                if k + 1 < 2 * hops:
+            landed(recv.at[k, piece], second.at[k, :, piece] if k < hops else first.at[k - hops, :, piece])
+
+            @pl.when(piece < (pieces if k + 1 < hops else early if k + 1 < 2 * hops else 0))
+            def _():
+                for c in range(COLOURS):
                     gather(c, k + 1, piece).start()
-                if k:
-                    gather(c, k - 1, piece).wait_send()
+
             if k == 0:
 
                 @pl.when(piece == 0)
                 def _():
                     gather(last, 0, pieces - 1).start()
 
-    @pl.loop(0, pieces)
-    def _(piece):
+    for k in range(hops):
+        landed(send.at[k], second.at[k])
+        landed(send.at[k + hops], first.at[k, :, pl.ds(0, early)])
+    landed(sq_send.at[0], squares.at[pl.ds(1, n - 1)])
+
+
+def last_kernel(side, layers, whole, after, out, local, send, recv):
+    pieces, tiles, hops = whole.shape[0], whole.shape[3], side - 1
+    part = tiles // COLOURS
+    me = lax.axis_index("dp")
+    x, y = me // side, me % side
+
+    def row(c, ref, piece, p):
+        cut = pl.ds(c * part, part)
+        return ref.at[piece, p, :, cut] if c < 2 else ref.at[piece, :, p, cut]
+
+    def ahead(c, i):
+        p, q = (x, y) if c < 2 else (y, x)
+        p = (p + i * (1 if c % 2 == 0 else -1) + 2 * side) % side
+        return p, {"dp": p * side + q if c < 2 else q * side + p}
+
+    def own(c, piece):
+        p = ahead(c, 0)[0]
+        return row(c, whole, pieces - layers + piece, p), row(c, out, piece, p)
+
+    def gather(c, k, piece):
+        moved = row(c, out, piece, ahead(c, -k)[0])
+        return pltpu.make_async_remote_copy(
+            src_ref=own(c, piece)[0] if k == 0 else moved, dst_ref=moved, send_sem=send.at[k], recv_sem=recv.at[k, piece], device_id=ahead(c, 1)[1], device_id_type=MESH
+        )
+
+    barrier = pltpu.get_barrier_semaphore()
+    for c in range(COLOURS):
+        pl.semaphore_signal(barrier, inc=1, device_id=ahead(c, 1)[1], device_id_type=MESH)
+    pl.semaphore_wait(barrier, COLOURS)
+
+    for piece in range(layers):
         for c in range(COLOURS):
-            gather(c, 2 * hops - 1, piece).wait_send()
-
-    @pl.loop(1, n)
-    def _(i):
-        tell(i).wait_send()
+            gather(c, 0, piece).start()
+    for piece in range(layers):
+        for c in range(COLOURS):
+            pltpu.make_async_copy(*own(c, piece), local.at[0]).start()
+    for k in range(hops):
+        for piece in range(layers):
+            pltpu.make_async_copy(out.at[0, 0], out.at[0, 0], recv.at[k, piece]).wait()
+            if k + 1 < hops:
+                for c in range(COLOURS):
+                    gather(c, k + 1, piece).start()
+    for k in range(hops):
+        pltpu.make_async_copy(out.at[:, 0], out.at[:, 0], send.at[k]).wait()
+    pltpu.make_async_copy(out.at[:, 0], out.at[:, 0], local.at[0]).wait()
 
 
 def out_kernel(layers, state, whole, *refs):
-    outs, sems = refs[:9], refs[9]
-    copies = [
-        pltpu.make_async_copy(source.at[piece], outs[3 * i + piece // layers].at[piece % layers], sems.at[i, piece])
-        for i, source in enumerate((whole, state.at[0], state.at[1]))
-        for piece in range(3 * layers)
+    outs, done, sems = refs[:8], refs[8], refs[9]
+    early = whole.shape[0] - layers
+    done[...] = jnp.zeros_like(done)
+    copies = [pltpu.make_async_copy(whole.at[i], outs[i // layers].at[i % layers], sems.at[0]) for i in range(early)]
+    copies += [
+        pltpu.make_async_copy(state.at[j, i], outs[2 + 3 * j + i // layers].at[i % layers], sems.at[1])
+        for j in range(2)
+        for i in range(3 * layers)
     ]
     for copy in copies:
         copy.start()
-    for copy in copies:
-        copy.wait()
+    for i, all_of_it in enumerate((whole.at[pl.ds(0, early)], state)):
+        pltpu.make_async_copy(all_of_it, all_of_it, sems.at[i]).wait()
+
+
+def last_out_kernel(last, out, sem):
+    copy = pltpu.make_async_copy(last, out, sem)
+    copy.start()
+    copy.wait()
 
 
 def solution(mesh):
@@ -276,27 +331,46 @@
                 pltpu.VMEM((pieces, tiles, 8, 128), bf16),
                 pltpu.VMEM((n, 8, 128), f32),
                 pltpu.VMEM((8, 128), f32),
-                dma((pieces,)),
-                dma((3, pieces)),
-                dma((2 * hops, COLOURS, pieces)),
-                dma((2 * hops, COLOURS, pieces)),
-                dma((n,)),
-                dma((n,)),
+                dma((1,)),
+                dma((2,)),
+                dma((2 * hops,)),
+                dma((2 * hops, pieces)),
+                dma((1,)),
+                dma((1,)),
             ],
             compiler_params=pltpu.CompilerParams(collective_id=0, has_side_effects=True, vmem_limit_bytes=27 * 2**20),
             name="step",
         )(*terms, *whole, *ms, *vs)
-        new = [pltpu.with_memory_space_constraint(one, pltpu.VMEM) for one in new]
-        shapes = [(layers, side, side, tiles, 8, 128)] * 3 + [(layers, tiles, 8, 128)] * 6
-        outs = pl.pallas_call(
+        state, gathered = (pltpu.with_memory_space_constraint(one, pltpu.VMEM) for one in new)
+        one, block = (layers, side, side, tiles, 8, 128), (layers, tiles, 8, 128)
+        *outs, after = pl.pallas_call(
             functools.partial(out_kernel, layers),
-            out_shape=[jax.ShapeDtypeStruct(s, bf16 if i < 3 else f32) for i, s in enumerate(shapes)],
+            out_shape=[jax.ShapeDtypeStruct(one, bf16)] * 2 + [jax.ShapeDtypeStruct(block, f32)] * 6 + [jax.ShapeDtypeStruct((8, 128), f32)],
             in_specs=[vmem] * 2,
-            out_specs=[any_space] * 9,
-            scratch_shapes=[dma((3, pieces))],
+            out_specs=[any_space] * 8 + [vmem],
+            scratch_shapes=[dma((2,))],
             compiler_params=pltpu.CompilerParams(vmem_limit_bytes=2**20),
             name="out",
-        )(*new)
+        )(state, gathered)
+        last = pl.pallas_call(
+            functools.partial(last_kernel, side, layers),
+            out_shape=pltpu.VMEM(one, bf16),
+            in_specs=[vmem, any_space],
+            out_specs=vmem,
+            scratch_shapes=[dma((1,)), dma((hops,)), dma((hops, layers))],
+            compiler_params=pltpu.CompilerParams(collective_id=1, has_side_effects=True, vmem_limit_bytes=2**20),
+            name="last",
+        )(gathered, after)
+        last = pl.pallas_call(
+            last_out_kernel,
+            out_shape=jax.ShapeDtypeStruct(one, bf16),
+            in_specs=[vmem],
+            out_specs=any_space,
+            scratch_shapes=[dma],
+            compiler_params=pltpu.CompilerParams(vmem_limit_bytes=2**20),
+            name="last_out",
+        )(pltpu.with_memory_space_constraint(last, pltpu.VMEM))
+        outs = [*outs[:2], last, *outs[2:]]
         return tuple(untiled(one, like.shape) for one, like in zip(outs, (*weights, *m, *v), strict=True))
 
     all_of, cut = P(None, None, None), P(None, "dp", None)

time: 305 us -> 290 us (0.951)
  Pallas kernels: 305 us -> 289 us
    pallas_call x1, Pallas kernels: 293 us -> 251 us  [step(): pl.pallas_call(functools.partial(step_kernel, side, layers, count), out_s...]
    pallas_call x0 -> x2, Pallas kernels: none -> 29.9 us  [the longest x1 26.2 us: step(): pl.pallas_call(functools.partial(last_kernel, side, layers), out_shape=pl...]
where the time goes in v4:
time: 290 us
  Pallas kernels  289 us (100%)
    pallas_call x1, Pallas kernels, step(): pl.pallas_call(functools.partial(step_kernel, side, layers, count), out_s...  251 us
    pallas_call x1, Pallas kernels, step(): pl.pallas_call(functools.partial(last_kernel, side, layers), out_shape=pl...  26.2 us
    pallas_call x1, Pallas kernels, step(): pl.pallas_call(functools.partial(out_kernel, layers), out_shape=[jax.Shap...  8.37 us

profile of v4, /device:TPU:96, one launch (start us, length us, event | category | flops | bytes accessed | tf_op | source)
XLA Modules:
  0.0 289.6 jit_solution(17040742028761392319)
XLA Ops:
  0.6 250.7 %step.1 = (f32[2,6,140,8,128]{4,3,2,1,0:T(8,128)S(1)}, bf16[6,4,4,140,8,128]{5,4,3,2,1,0:T(8,128)(2,1)S(1)}) custom-call(bf16[2,4,4,140,8,128]{5,4,3,2,1,0:T(8,128)(2,1)} %bitcast.106, bf16[2,4,4,140,8,128]{5,4,3,2,1,0:T(8,128)(2,1)} %bitcast.107, bf16[2,4,4,140,8,128]{5,4,3,2,1,0:T(8,128)(2,1)} %bitcast.108, bf16[2,4,4,140,8,128]{5,4,3,2,1,0:T(8,128)(2,1)} %bitcast.109, ...), custom_call_target="tpu_custom_call" | custom-call | tf_op jit(solution)/shard_map/step/pallas_call | solution.py:320
  251.4 8.4 %out.1 = (bf16[2,4,4,140,8,128]{5,4,3,2,1,0:T(8,128)(2,1)}, bf16[2,4,4,140,8,128]{5,4,3,2,1,0:T(8,128)(2,1)}, f32[2,140,8,128]{3,2,1,0:T(8,128)}, f32[2,140,8,12...) custom-call(f32[2,6,140,8,128]{4,3,2,1,0:T(8,128)S(1)} %get-tuple-el, ...), custom_call_target="tpu_custom_call" | custom-call | tf_op jit(solution)/shard_map/out/pallas_call | solution.py:346
  259.7 26.2 %last.1 = bf16[2,4,4,140,8,128]{5,4,3,2,1,0:T(8,128)(2,1)S(1)} custom-call(bf16[6,4,4,140,8,128]{5,4,3,2,1,0:T(8,128)(2,1)S(1)} %get-tuple-element.21.whole, f32[8,128]{1,0:T(8,128)S(1)} %get-tuple-element.24.after), custom_call_target="tpu_custom_call" | custom-call | tf_op jit(solution)/shard_map/last/pallas_call | solution.py:355
  285.9 3.7 %last_out.1 = bf16[2,4,4,140,8,128]{5,4,3,2,1,0:T(8,128)(2,1)} custom-call(bf16[2,4,4,140,8,128]{5,4,3,2,1,0:T(8,128)(2,1)S(1)} %last.1), custom_call_target="tpu_custom_call" | custom-call | tf_op jit(solution)/shard_map/last_out/pallas_call | solution.py:364

commit v5 on v4

--- a/solution.py
+++ b/solution.py
@@ -228,7 +228,7 @@
     landed(sq_send.at[0], squares.at[pl.ds(1, n - 1)])
 
 
-def last_kernel(side, layers, whole, after, out, local, send, recv):
+def last_kernel(side, layers, whole, after, out, send, recv):
     pieces, tiles, hops = whole.shape[0], whole.shape[3], side - 1
     part = tiles // COLOURS
     me = lax.axis_index("dp")
@@ -261,9 +261,6 @@
     for piece in range(layers):
         for c in range(COLOURS):
             gather(c, 0, piece).start()
-    for piece in range(layers):
-        for c in range(COLOURS):
-            pltpu.make_async_copy(*own(c, piece), local.at[0]).start()
     for k in range(hops):
         for piece in range(layers):
             pltpu.make_async_copy(out.at[0, 0], out.at[0, 0], recv.at[k, piece]).wait()
@@ -272,29 +269,45 @@
                     gather(c, k + 1, piece).start()
     for k in range(hops):
         pltpu.make_async_copy(out.at[:, 0], out.at[:, 0], send.at[k]).wait()
-    pltpu.make_async_copy(out.at[:, 0], out.at[:, 0], local.at[0]).wait()
-
-
-def out_kernel(layers, state, whole, *refs):
-    outs, done, sems = refs[:8], refs[8], refs[9]
+
+
+def row_of(side, c, ref, piece, i):
+    part = ref.shape[3] // COLOURS
+    me = lax.axis_index("dp")
+    p = ((me // side if c < 2 else me % side) + i * (1 if c % 2 == 0 else -1) + 2 * side) % side
+    cut = pl.ds(c * part, part)
+    return ref.at[piece, p, :, cut] if c < 2 else ref.at[piece, :, p, cut]
+
+
+def out_kernel(side, layers, state, whole, *refs):
+    outs, done, sems = refs[:9], refs[9], refs[10]
     early = whole.shape[0] - layers
     done[...] = jnp.zeros_like(done)
     copies = [pltpu.make_async_copy(whole.at[i], outs[i // layers].at[i % layers], sems.at[0]) for i in range(early)]
     copies += [
-        pltpu.make_async_copy(state.at[j, i], outs[2 + 3 * j + i // layers].at[i % layers], sems.at[1])
+        pltpu.make_async_copy(row_of(side, c, whole, early + i, 0), row_of(side, c, outs[2], i, 0), sems.at[2])
+        for i in range(layers)
+        for c in range(COLOURS)
+    ]
+    copies += [
+        pltpu.make_async_copy(state.at[j, i], outs[3 + 3 * j + i // layers].at[i % layers], sems.at[1])
         for j in range(2)
         for i in range(3 * layers)
     ]
     for copy in copies:
         copy.start()
-    for i, all_of_it in enumerate((whole.at[pl.ds(0, early)], state)):
+    for i, all_of_it in enumerate((whole.at[pl.ds(0, early)], state, whole.at[pl.ds(0, layers), 0])):
         pltpu.make_async_copy(all_of_it, all_of_it, sems.at[i]).wait()
 
 
-def last_out_kernel(last, out, sem):
-    copy = pltpu.make_async_copy(last, out, sem)
-    copy.start()
-    copy.wait()
+def last_out_kernel(side, last, so_far, out, sem):
+    layers = last.shape[0]
+    for piece in range(layers):
+        for c in range(COLOURS):
+            for i in range(1, side):
+                pltpu.make_async_copy(row_of(side, c, last, piece, i), row_of(side, c, out, piece, i), sem).start()
+    others = last.at[:, pl.ds(1, side - 1)]
+    pltpu.make_async_copy(others, others, sem).wait()
 
 
 def solution(mesh):
@@ -344,11 +357,11 @@
         state, gathered = (pltpu.with_memory_space_constraint(one, pltpu.VMEM) for one in new)
         one, block = (layers, side, side, tiles, 8, 128), (layers, tiles, 8, 128)
         *outs, after = pl.pallas_call(
-            functools.partial(out_kernel, layers),
-            out_shape=[jax.ShapeDtypeStruct(one, bf16)] * 2 + [jax.ShapeDtypeStruct(block, f32)] * 6 + [jax.ShapeDtypeStruct((8, 128), f32)],
+            functools.partial(out_kernel, side, layers),
+            out_shape=[jax.ShapeDtypeStruct(one, bf16)] * 3 + [jax.ShapeDtypeStruct(block, f32)] * 6 + [jax.ShapeDtypeStruct((8, 128), f32)],
             in_specs=[vmem] * 2,
-            out_specs=[any_space] * 8 + [vmem],
-            scratch_shapes=[dma((2,))],
+            out_specs=[any_space] * 9 + [vmem],
+            scratch_shapes=[dma((3,))],
             compiler_params=pltpu.CompilerParams(vmem_limit_bytes=2**20),
             name="out",
         )(state, gathered)
@@ -357,20 +370,20 @@
             out_shape=pltpu.VMEM(one, bf16),
             in_specs=[vmem, any_space],
             out_specs=vmem,
-            scratch_shapes=[dma((1,)), dma((hops,)), dma((hops, layers))],
+            scratch_shapes=[dma((hops,)), dma((hops, layers))],
             compiler_params=pltpu.CompilerParams(collective_id=1, has_side_effects=True, vmem_limit_bytes=2**20),
             name="last",
         )(gathered, after)
-        last = pl.pallas_call(
-            last_out_kernel,
+        outs[2] = pl.pallas_call(
+            functools.partial(last_out_kernel, side),
             out_shape=jax.ShapeDtypeStruct(one, bf16),
-            in_specs=[vmem],
+            in_specs=[vmem, any_space],
             out_specs=any_space,
+            input_output_aliases={1: 0},
             scratch_shapes=[dma],
             compiler_params=pltpu.CompilerParams(vmem_limit_bytes=2**20),
             name="last_out",
-        )(pltpu.with_memory_space_constraint(last, pltpu.VMEM))
-        outs = [*outs[:2], last, *outs[2:]]
+        )(pltpu.with_memory_space_constraint(last, pltpu.VMEM), outs[2])
         return tuple(untiled(one, like.shape) for one, like in zip(outs, (*weights, *m, *v), strict=True))
 
     all_of, cut = P(None, None, None), P(None, "dp", None)

time: 290 us -> 289 us (level)
  no operation moved by 1% of the time
where the time goes in v5:
time: 289 us
  Pallas kernels  288 us (100%)
    pallas_call x1, Pallas kernels, step(): pl.pallas_call(functools.partial(step_kernel, side, layers, count), out_s...  250 us
    pallas_call x1, Pallas kernels, step(): pl.pallas_call(functools.partial(last_kernel, side, layers), out_shape=pl...  26.2 us
    pallas_call x1, Pallas kernels, step(): pl.pallas_call(functools.partial(out_kernel, side, layers), out_shape=[ja...  9.07 us

profile of v5, /device:TPU:96, one launch (start us, length us, event | category | flops | bytes accessed | tf_op | source)
XLA Modules:
  0.0 288.8 jit_solution(5421245406923333718)
XLA Ops:
  0.6 250.0 %step.1 = (f32[2,6,140,8,128]{4,3,2,1,0:T(8,128)S(1)}, bf16[6,4,4,140,8,128]{5,4,3,2,1,0:T(8,128)(2,1)S(1)}) custom-call(bf16[2,4,4,140,8,128]{5,4,3,2,1,0:T(8,128)(2,1)} %bitcast.106, bf16[2,4,4,140,8,128]{5,4,3,2,1,0:T(8,128)(2,1)} %bitcast.107, bf16[2,4,4,140,8,128]{5,4,3,2,1,0:T(8,128)(2,1)} %bitcast.108, bf16[2,4,4,140,8,128]{5,4,3,2,1,0:T(8,128)(2,1)} %bitcast.109, ...), custom_call_target="tpu_custom_call" | custom-call | tf_op jit(solution)/shard_map/step/pallas_call | solution.py:333
  250.7 9.1 %out.1 = (bf16[2,4,4,140,8,128]{5,4,3,2,1,0:T(8,128)(2,1)}, bf16[2,4,4,140,8,128]{5,4,3,2,1,0:T(8,128)(2,1)}, bf16[2,4,4,140,8,128]{5,4,3,2,1,0:T(8,128)(2,1)}, ...) custom-call(f32[2,6,140,8,128]{4,3,2,1,0:T(8,128)S(1)} %get-tuple-el, ...), custom_call_target="tpu_custom_call" | custom-call | tf_op jit(solution)/shard_map/out/pallas_call | solution.py:359
  259.7 26.2 %last.1 = bf16[2,4,4,140,8,128]{5,4,3,2,1,0:T(8,128)(2,1)S(1)} custom-call(bf16[6,4,4,140,8,128]{5,4,3,2,1,0:T(8,128)(2,1)S(1)} %get-tuple-element.22.whole, f32[8,128]{1,0:T(8,128)S(1)} %get-tuple-element.25.after), custom_call_target="tpu_custom_call" | custom-call | tf_op jit(solution)/shard_map/last/pallas_call | solution.py:368
  285.9 2.8 last_out.1
